TPU v7x, 32 devices: a whole 2x2x4 slice. The times are simulated.
32 devices in a mesh: dp: 8 (over y, x, core), mp: 4 (over z).
Axes of the slice: x: 2, y: 2, z: 4, core: 2. Of those that a mesh axis runs over, the one named last changes fastest.
Arguments:
- tokens: bfloat16 [8192, 2048], P('dp'), may hold values from -6 to 6
- doc_lengths: int32 [8, 8], P('dp'), may hold values from 1 to 512, 1024 in all within a row
- slot_live: int32 [36], P('mp'), may hold values from 0 to 1, as said below
- attn_gain: bfloat16 [2048], replicated, may hold values from 0.5 to 1.5
- w_query: bfloat16 [2048, 1536], P(None, 'mp'), may hold values from -0.125 to 0.125
- w_keyval: bfloat16 [2048, 768], replicated, may hold values from -0.125 to 0.125
- q_gain: bfloat16 [64], replicated, may hold values from 0.099609375 to 1.8984375
- k_gain: bfloat16 [64], replicated, may hold values from 0.099609375 to 1.8984375
- w_out: bfloat16 [1536, 2048], P('mp'), may hold values from -0.625 to 0.625
- ffn_gain: bfloat16 [2048], replicated, may hold values from 0.5 to 1.5
- w_gate: bfloat16 [2048, 4608], P(None, 'mp'), may hold values from -0.125 to 0.125
- w_up: bfloat16 [2048, 4608], P(None, 'mp'), may hold values from -0.125 to 0.125
- w_down: bfloat16 [4608, 2048], P('mp'), may hold values from -0.09375 to 0.09375
- out_grad: bfloat16 [8192, 2048], P('dp'), may hold values from -6 to 6
Outputs:
- block_out: bfloat16 [8192, 2048], P(('dp', 'mp'))
- grad_tokens: float32 [8192, 2048], P(('dp', 'mp'))
- grad_attn_gain: float32 [2048], replicated
- grad_query: float32 [2048, 1536], P('dp', 'mp')
- grad_keyval: float32 [2048, 768], P(('dp', 'mp'))
- grad_q_gain: float32 [64], replicated
- grad_k_gain: float32 [64], replicated
- grad_out_proj: float32 [1536, 2048], P('mp', 'dp')
- grad_ffn_gain: float32 [2048], replicated
- grad_gate: float32 [2048, 4608], P('dp', 'mp')
- grad_up: float32 [2048, 4608], P('dp', 'mp')
- grad_down: float32 [4608, 2048], P('mp', 'dp')
Inputs may be any that keep to these rules, and one draw needn't show every extreme that they name: `doc_lengths`: each row's 8 lengths sum to 1024, and one of them is 512. `slot_live`: the 9 slots of each index of mp hold 34 // 4 or 34 // 4 + 1 live ones, 34 live in all; which slots and which indices hold more varies.
All inputs are finite; a program needn't handle non-finite values.
Results may differ from a plain program's by a relative error of at most 0.018.
Values may be sent and summed in bfloat16 or wider, within the bound.
A program may use at most 192 MiB of HBM per device.

v0:
```python
import math
import jax
import jax.numpy as jnp
from jax import lax
from jax.sharding import PartitionSpec as P

EPSILON = 1e-06
MASKED = -1000000000.0
ROPE_BASE = 10000.0
HIGHEST_PREC = lax.Precision.HIGHEST
CONTRACT_LAST = (((1,), (1,)), ((), ()))
CONTRACT_FIRST = (((0,), (0,)), ((), ()))


def normalize(raw_in):
    return raw_in * lax.rsqrt(jnp.mean(raw_in * raw_in, axis=-1, keepdims=True) + EPSILON)


def norm_back(grad_normed, raw_in, gain_vec):
    factor = lax.rsqrt(jnp.mean(raw_in * raw_in, axis=-1, keepdims=True) + EPSILON)
    unit_rows = raw_in * factor
    scaled = grad_normed * gain_vec
    grad_raw = factor * (scaled - unit_rows * jnp.mean(scaled * unit_rows, axis=-1, keepdims=True))
    return (grad_raw, jnp.sum(grad_normed * unit_rows, axis=tuple(range(raw_in.ndim - 1))))


def rotate(values, cosine_tab, sine_tab, sign):
    half_size = values.shape[-1] // 2
    first_half = values[..., :half_size]
    second_half = values[..., half_size:]
    return jnp.concatenate(
        [
            first_half * cosine_tab - sign * second_half * sine_tab,
            second_half * cosine_tab + sign * first_half * sine_tab,
        ],
        axis=-1,
    )


def doc_layout(lengths, row_count):
    doc_ends = jnp.cumsum(lengths)
    token_index = jnp.arange(row_count, dtype=jnp.int32)
    past_end = (token_index[:, None] >= doc_ends[None, :]).astype(jnp.int32)
    doc_id = jnp.sum(past_end, axis=1)
    doc_pos = token_index - jnp.sum(past_end * lengths[None, :], axis=1)
    return (doc_id, doc_pos, token_index)


def rope_table(doc_pos, head_size):
    rope_freq = jnp.exp(
        jnp.arange(head_size // 2, dtype=jnp.float32) * (-2.0 * math.log(ROPE_BASE) / head_size)
    )
    rope_angle = doc_pos.astype(jnp.float32)[:, None] * rope_freq[None, :]
    return (jnp.cos(rope_angle)[:, None, :], jnp.sin(rope_angle)[:, None, :])


def shards(
    tokens,
    doc_lengths,
    slot_live,
    attn_gain,
    w_query,
    w_keyval,
    q_gain,
    k_gain,
    w_out,
    ffn_gain,
    w_gate,
    w_up,
    w_down,
    out_grad,
):
    row_count, model_width = tokens.shape
    head_size = q_gain.shape[0]
    heads_dev = w_query.shape[1] // head_size
    heads_all = heads_dev * lax.axis_size("mp")
    kv_heads = w_keyval.shape[1] // (2 * head_size)
    group_size = heads_all // kv_heads
    kv_window = min(kv_heads, (heads_dev + group_size - 2) // group_size + 1)
    tile_cols = w_gate.shape[1] // slot_live.shape[0]
    shard_rows = row_count // lax.axis_size("mp")
    block_rows = min(512, row_count)
    score_scale = head_size ** (-0.5)
    head_span = heads_dev * head_size
    mp_index = lax.axis_index("mp")
    row_first = mp_index * shard_rows
    q_first = mp_index * heads_dev
    kv_first = jnp.minimum(q_first // group_size, kv_heads - kv_window)
    kv_owner = (q_first + jnp.arange(heads_dev, dtype=jnp.int32)) // group_size - kv_first
    head_pick = (kv_owner[:, None] == jnp.arange(kv_window, dtype=jnp.int32)[None, :]).astype(
        jnp.float32
    )
    key_cols = lax.dynamic_slice_in_dim(w_keyval, kv_first * head_size, kv_window * head_size, 1)
    value_cols = lax.dynamic_slice_in_dim(
        w_keyval, (kv_heads + kv_first) * head_size, kv_window * head_size, 1
    )

    def spread(window_cols):
        return (
            jnp.einsum(
                "dwe,hw->dhe",
                window_cols.reshape(model_width, kv_window, head_size),
                head_pick.astype(jnp.bfloat16),
                preferred_element_type=jnp.float32,
            )
            .astype(jnp.bfloat16)
            .reshape(model_width, head_span)
        )

    def fold_heads(per_head):
        return jnp.einsum(
            "dhe,hw->dwe",
            per_head.reshape(model_width, heads_dev, head_size),
            head_pick,
            precision=HIGHEST_PREC,
        ).reshape(model_width, kv_window * head_size)

    doc_id, doc_pos, token_index = doc_layout(doc_lengths[0], row_count)
    cosine_tab, sine_tab = rope_table(doc_pos, head_size)
    x_float = tokens.astype(jnp.float32)
    x_rows = lax.dynamic_slice_in_dim(x_float, row_first, shard_rows, 0)
    gain_one = attn_gain.astype(jnp.float32)
    gain_two = ffn_gain.astype(jnp.float32)
    q_gain_f = q_gain.astype(jnp.float32)
    k_gain_f = k_gain.astype(jnp.float32)
    xn_one = (normalize(x_float) * gain_one).astype(jnp.bfloat16)
    q_raw = jnp.dot(xn_one, w_query, preferred_element_type=jnp.float32).reshape(
        row_count, heads_dev, head_size
    )
    kv_raw = jnp.dot(
        xn_one, jnp.concatenate([key_cols, value_cols], axis=1), preferred_element_type=jnp.float32
    ).reshape(row_count, 2, kv_window, head_size)
    k_raw = jnp.einsum("twe,hw->the", kv_raw[:, 0], head_pick, precision=HIGHEST_PREC)
    v_raw = jnp.einsum("twe,hw->the", kv_raw[:, 1], head_pick, precision=HIGHEST_PREC)
    q_rot = rotate(normalize(q_raw) * q_gain_f, cosine_tab, sine_tab, 1.0).astype(jnp.bfloat16)
    k_rot = rotate(normalize(k_raw) * k_gain_f, cosine_tab, sine_tab, 1.0).astype(jnp.bfloat16)
    v_low = v_raw.astype(jnp.bfloat16)

    def block_scores(row_start, key_stop):
        scores = (
            jnp.einsum(
                "qhe,khe->hqk",
                q_rot[row_start : row_start + block_rows],
                k_rot[:key_stop],
                preferred_element_type=jnp.float32,
            )
            * score_scale
        )
        allowed = (doc_id[row_start : row_start + block_rows, None] == doc_id[None, :key_stop]) & (
            token_index[None, :key_stop] <= token_index[row_start : row_start + block_rows, None]
        )
        return jnp.where(allowed[None], scores, MASKED)

    block_outs = []
    block_lse = []
    for row_start in range(0, row_count, block_rows):
        key_stop = row_start + block_rows
        scores = block_scores(row_start, key_stop)
        row_max = jnp.max(scores, axis=-1, keepdims=True)
        shifted = jnp.exp(scores - row_max)
        row_total = jnp.sum(shifted, axis=-1, keepdims=True)
        attn_probs = (shifted / row_total).astype(jnp.bfloat16)
        block_outs.append(
            jnp.einsum(
                "hqk,khe->qhe", attn_probs, v_low[:key_stop], preferred_element_type=jnp.float32
            )
        )
        block_lse.append(row_max + jnp.log(row_total))
    attended = (
        jnp.concatenate(block_outs, axis=0).reshape(row_count, head_span).astype(jnp.bfloat16)
    )
    attn_part = jnp.dot(attended, w_out, preferred_element_type=jnp.float32)
    hidden_full = x_float + lax.psum(attn_part, "mp")
    hidden_rows = lax.dynamic_slice_in_dim(hidden_full, row_first, shard_rows, 0)
    xn_two = (normalize(hidden_full) * gain_two).astype(jnp.bfloat16)
    live_cols = jnp.repeat(slot_live.astype(jnp.float32), tile_cols)
    gate_act = jnp.dot(xn_two, w_gate, preferred_element_type=jnp.float32)
    up_act = jnp.dot(xn_two, w_up, preferred_element_type=jnp.float32)
    gate_sigmoid = jax.nn.sigmoid(gate_act)
    gate_silu = gate_act * gate_sigmoid
    ffn_hidden = (gate_silu * up_act * live_cols).astype(jnp.bfloat16)
    ffn_part = jnp.dot(ffn_hidden, w_down, preferred_element_type=jnp.float32)
    out_rows = hidden_rows + lax.psum_scatter(
        ffn_part.astype(jnp.bfloat16), "mp", scatter_dimension=0, tiled=True
    ).astype(jnp.float32)
    block_out = out_rows.astype(jnp.bfloat16)
    d_hidden = (
        lax.dot_general(out_grad, w_down, CONTRACT_LAST, preferred_element_type=jnp.float32)
        * live_cols
    )
    grad_down = lax.dot_general(
        ffn_hidden, out_grad, CONTRACT_FIRST, preferred_element_type=jnp.float32
    )
    d_gate = (d_hidden * up_act * gate_sigmoid * (1.0 + gate_act * (1.0 - gate_sigmoid))).astype(
        jnp.bfloat16
    )
    d_up = (d_hidden * gate_silu).astype(jnp.bfloat16)
    grad_gate = lax.dot_general(xn_two, d_gate, CONTRACT_FIRST, preferred_element_type=jnp.float32)
    grad_up = lax.dot_general(xn_two, d_up, CONTRACT_FIRST, preferred_element_type=jnp.float32)
    dn_two_part = lax.dot_general(
        d_gate, w_gate, CONTRACT_LAST, preferred_element_type=jnp.float32
    ) + lax.dot_general(d_up, w_up, CONTRACT_LAST, preferred_element_type=jnp.float32)
    dn_two = lax.psum(dn_two_part, "mp")
    back_two, _ = norm_back(dn_two, hidden_full, gain_two)
    dh_full = out_grad.astype(jnp.float32) + back_two
    dh_rows = lax.dynamic_slice_in_dim(dh_full, row_first, shard_rows, 0)
    grad_gain_two = jnp.sum(
        lax.dynamic_slice_in_dim(dn_two, row_first, shard_rows, 0) * normalize(hidden_rows), axis=0
    )
    dh_low = dh_full.astype(jnp.bfloat16)
    grad_out_proj = lax.dot_general(
        attended, dh_low, CONTRACT_FIRST, preferred_element_type=jnp.float32
    )
    d_att = lax.dot_general(dh_low, w_out, CONTRACT_LAST, preferred_element_type=jnp.float32)
    d_att = d_att.astype(jnp.bfloat16).reshape(row_count, heads_dev, head_size)
    dq_blocks = []
    d_keys = jnp.zeros((row_count, heads_dev, head_size), jnp.float32)
    d_values = jnp.zeros((row_count, heads_dev, head_size), jnp.float32)
    for block_index, row_start in enumerate(range(0, row_count, block_rows)):
        key_stop = row_start + block_rows
        scores = block_scores(row_start, key_stop)
        attn_probs = jnp.exp(scores - block_lse[block_index])
        probs_low = attn_probs.astype(jnp.bfloat16)
        att_rows = d_att[row_start:key_stop]
        d_probs = jnp.einsum(
            "qhe,khe->hqk", att_rows, v_low[:key_stop], preferred_element_type=jnp.float32
        )
        d_scores = (
            attn_probs * (d_probs - jnp.sum(d_probs * attn_probs, axis=-1, keepdims=True))
        ).astype(jnp.bfloat16)
        dq_blocks.append(
            jnp.einsum(
                "hqk,khe->qhe", d_scores, k_rot[:key_stop], preferred_element_type=jnp.float32
            )
            * score_scale
        )
        d_keys = d_keys.at[:key_stop].add(
            jnp.einsum(
                "hqk,qhe->khe",
                d_scores,
                q_rot[row_start:key_stop],
                preferred_element_type=jnp.float32,
            )
            * score_scale
        )
        d_values = d_values.at[:key_stop].add(
            jnp.einsum("hqk,qhe->khe", probs_low, att_rows, preferred_element_type=jnp.float32)
        )
    d_queries = jnp.concatenate(dq_blocks, axis=0)
    dq_raw, grad_q_gain = norm_back(rotate(d_queries, cosine_tab, sine_tab, -1.0), q_raw, q_gain_f)
    dk_raw, grad_k_gain = norm_back(rotate(d_keys, cosine_tab, sine_tab, -1.0), k_raw, k_gain_f)
    d_proj = jnp.concatenate(
        [
            dq_raw.reshape(row_count, head_span),
            dk_raw.reshape(row_count, head_span),
            d_values.reshape(row_count, head_span),
        ],
        axis=1,
    ).astype(jnp.bfloat16)
    w_proj = jnp.concatenate([w_query, spread(key_cols), spread(value_cols)], axis=1)
    dn_one_part = lax.dot_general(d_proj, w_proj, CONTRACT_LAST, preferred_element_type=jnp.float32)
    grad_proj = lax.dot_general(xn_one, d_proj, CONTRACT_FIRST, preferred_element_type=jnp.float32)
    grad_query = grad_proj[:, :head_span]
    grad_keyval = jnp.zeros((model_width, 2 * kv_heads * head_size), jnp.float32)
    grad_keyval = lax.dynamic_update_slice_in_dim(
        grad_keyval, fold_heads(grad_proj[:, head_span : 2 * head_span]), kv_first * head_size, 1
    )
    grad_keyval = lax.dynamic_update_slice_in_dim(
        grad_keyval, fold_heads(grad_proj[:, 2 * head_span :]), (kv_heads + kv_first) * head_size, 1
    )
    dn_one_rows = lax.psum_scatter(
        dn_one_part.astype(jnp.bfloat16), "mp", scatter_dimension=0, tiled=True
    ).astype(jnp.float32)
    back_one, grad_gain_one = norm_back(dn_one_rows, x_rows, gain_one)
    grad_tokens = dh_rows + back_one
    grad_query, grad_out_proj, grad_gate, grad_up, grad_down = (
        lax.psum_scatter(
            grad_query.astype(jnp.bfloat16), "dp", scatter_dimension=0, tiled=True
        ).astype(jnp.float32),
        lax.psum_scatter(
            grad_out_proj.astype(jnp.bfloat16), "dp", scatter_dimension=1, tiled=True
        ).astype(jnp.float32),
        lax.psum_scatter(
            grad_gate.astype(jnp.bfloat16), "dp", scatter_dimension=0, tiled=True
        ).astype(jnp.float32),
        lax.psum_scatter(
            grad_up.astype(jnp.bfloat16), "dp", scatter_dimension=0, tiled=True
        ).astype(jnp.float32),
        lax.psum_scatter(
            grad_down.astype(jnp.bfloat16), "dp", scatter_dimension=1, tiled=True
        ).astype(jnp.float32),
    )
    grad_keyval = lax.psum_scatter(grad_keyval, ("dp", "mp"), scatter_dimension=0, tiled=True)
    grad_gain_one, grad_gain_two, grad_q_gain, grad_k_gain = lax.psum(
        (grad_gain_one, grad_gain_two, grad_q_gain, grad_k_gain), ("dp", "mp")
    )
    return (
        block_out,
        grad_tokens,
        grad_gain_one,
        grad_query,
        grad_keyval,
        grad_q_gain,
        grad_k_gain,
        grad_out_proj,
        grad_gain_two,
        grad_gate,
        grad_up,
        grad_down,
    )


def solution(mesh):
    return jax.shard_map(
        shards,
        mesh=mesh,
        in_specs=(
            P("dp", None),
            P("dp", None),
            P("mp"),
            P(),
            P(None, "mp"),
            P(),
            P(),
            P(),
            P("mp", None),
            P(),
            P(None, "mp"),
            P(None, "mp"),
            P("mp", None),
            P("dp", None),
        ),
        out_specs=(
            P(("dp", "mp"), None),
            P(("dp", "mp"), None),
            P(),
            P("dp", "mp"),
            P(("dp", "mp"), None),
            P(),
            P(),
            P("mp", "dp"),
            P(),
            P("dp", "mp"),
            P("dp", "mp"),
            P("mp", "dp"),
        ),
        check_vma=False,
    )
```

profile of v0, /device:TPU:0, one launch (start us, length us, event | category | flops | bytes accessed | tf_op | source)
XLA Modules:
  0.0 1244.2 jit_solution(17080760547115743847)
XLA Ops:
  8.2 3.3 multiply_reduce_fusion.3
  11.6 3.5 fusion.103
  15.3 4.5 constant_dynamic-slice_fusion.1
  19.9 2.6 copy.165
  22.5 2.2 copy.164
  24.7 4.5 fusion.45
  34.5 2.9 fusion.58
  41.0 2.4 fusion.108
  43.5 3.0 fusion
  48.0 3.6 fusion.68
  56.8 5.6 fusion.110
  63.2 292.8 %all-reduce.6.cloned.1.call-done = f32[1024,2048]{1,0:T(8,128)} async-done(((f32[1024,2048]{1,0:T(8,128)}), f32[1024,2048]{1,0:T(8,128)}) %all-reduce.6.cloned.1.call-update) | async-done | bytes 8388624 | tf_op jit(solution)/shard_map/psum | solution.py:173
  356.0 5.7 multiply_reduce_fusion.2
  362.5 2.4 copy-done.2
  364.9 11.4 fusion.111
  376.4 7.3 fusion.112
  383.7 12.7 %multiply_convert_fusion.4 = (bf16[1024,1152]{1,0:T(8,128)(2,1)S(1)}, bf16[1024,1152]{1,0:T(8,128)(2,1)}, bf16[1024,1152]{1,0:T(8,128)(2,1)}) fusion(f32[1024,1152]{1,0:T(8,128)} %fusion.111, f32[1024,1152]{1,0:T(8,128)} %fusion.112, f32[1152]{0:T(1024)S(1)} %broadcast_bitcast_fusion, bf16[1024,2048]{1,0:T(8,128)(2,1)S(1)} %copy-done.27, ...), kind=kOutput, calls=%fused_computation.36 | convolution fusion | flops 4851892224 | bytes 25432576 | tf_op jit(solution)/shard_map/dot_general | solution.py:188
  396.5 8.1 fusion.113
  404.6 8.5 convolution_add_fusion
  413.3 9.6 convolution_convert_fusion.2
  422.9 9.6 convolution_convert_fusion.1
  432.6 9.2 convolution_convert_fusion
  442.5 9.5 convolution_convert_fusion.3
  452.1 251.1 %all-reduce.8.cloned.1.call-done = f32[1024,2048]{1,0:T(8,128)} async-done(((f32[1024,2048]{1,0:T(8,128)}), f32[1024,2048]{1,0:T(8,128)}) %all-reduce.8.cloned.1.call-update) | async-done | bytes 8388624 | tf_op jit(solution)/shard_map/psum | solution.py:203
  703.2 6.9 multiply_reduce_fusion.1
  713.0 8.3 multiply_add_fusion
  721.3 5.3 fusion.55
  727.4 4.7 multiply_reduce_fusion.4
  732.1 4.8 multiply_convert_fusion.3
  737.0 2.7 fusion.64
  739.6 2.9 fusion.62
  742.6 6.3 multiply_reduce_fusion
  748.9 6.9 multiply_convert_fusion
  757.1 2.1 fusion.63
  766.0 2.8 fusion.49
  768.8 5.3 fusion.73
  774.2 3.7 copy-done.14
  779.3 6.4 convolution_convert_fusion.6
  785.8 2.7 copy.152
  792.5 7.4 fusion.19
  800.1 5.2 fusion.104
  805.3 3.7 fusion.26
  811.8 5.7 fusion.29
  818.4 1.8 copy.158
  820.2 3.0 broadcast_in_dim.37
  823.2 11.5 dynamic_update_slice.6
  834.7 11.0 dynamic_update_slice.7
  845.8 6.5 convert_element_type.145
  852.3 1.8 multiply_reduce_fusion.7
  854.1 1.8 multiply_reduce_fusion.6
  856.0 2.2 convert_element_type.185
  858.1 2.2 convert_element_type.187
  860.3 13.2 %reduce-scatter.23.cloned.1.call-done = bf16[1152,256]{1,0:T(8,128)(2,1)} async-done(((bf16[1152,2048]{1,0:T(8,128)(2,1)}), bf16[1152,256]{1,0:T(8,128)(2,1)}) %reduce-scatter.23.cloned.1.call-update) | async-done | bytes 589840 | tf_op jit(solution)/shard_map/reduce_scatter | solution.py:289
  873.6 2.2 convert_element_type.189
  875.8 76.7 %reduce-scatter.9.cloned.1.call-done = bf16[256,2048]{1,0:T(8,128)(2,1)} async-done(((bf16[1024,2048]{1,0:T(8,128)(2,1)}), bf16[256,2048]{1,0:T(8,128)(2,1)}) %reduce-scatter.9.cloned.1.call-update) | async-done | bytes 1048592 | tf_op jit(solution)/shard_map/reduce_scatter | solution.py:183
  952.5 4.0 multiply_reduce_fusion.5
  956.6 38.2 %reduce-scatter.13.cloned.1.call-done = bf16[256,384]{0,1:T(8,128)(2,1)} async-done(((bf16[2048,384]{0,1:T(8,128)(2,1)}), bf16[256,384]{0,1:T(8,128)(2,1)}) %reduce-scatter.13.cloned.1.call-update) | async-done | bytes 196624 | tf_op jit(solution)/shard_map/reduce_scatter | solution.py:277
  994.7 1.8 copy.159
  996.5 39.9 %reduce-scatter.17.cloned.1.call-done = bf16[384,256]{1,0:T(8,128)(2,1)} async-done(((bf16[384,2048]{1,0:T(8,128)(2,1)}), bf16[384,256]{1,0:T(8,128)(2,1)}) %reduce-scatter.17.cloned.1.call-update) | async-done | bytes 196624 | tf_op jit(solution)/shard_map/reduce_scatter | solution.py:280
  1038.1 77.4 %reduce-scatter.11.cloned.1.call-done = bf16[256,2048]{1,0:T(8,128)(2,1)} async-done(((bf16[1024,2048]{1,0:T(8,128)(2,1)}), bf16[256,2048]{1,0:T(8,128)(2,1)}) %reduce-scatter.11.cloned.1.call-update) | async-done | bytes 1048592 | tf_op jit(solution)/shard_map/reduce_scatter | solution.py:271
  1115.5 2.7 fusion.39
  1118.2 41.1 %all-reduce.2 = (f32[2048]{0:T(1024)}, f32[64]{0:T(128)}, f32[64]{0:T(128)}, f32[2048]{0:T(1024)}) all-reduce(f32[2048]{0:T(1024)S(1)} %get-tuple-element.124, f32[64]{0:T(128)S(1)} %reduce_sum.217, f32[64]{0:T(128)S(1)} %get-tuple-element.126, f32[2048]{0:T(1024)S(1)} %get-tuple-element.141), channel_id=1, replica_groups=mesh['dp'=8,'mp'=4] {'dp','mp'}, use_global_device_ids=true, to_apply=%region_23.24 | all-reduce | flops 4224 | bytes 33792 | tf_op jit(solution)/shard_map/psum | solution.py:294
  1159.3 4.6 fusion.38
  1163.9 73.2 %reduce-scatter.15.cloned.1.call-done = f32[64,768]{1,0:T(8,128)} async-done(((f32[2048,768]{1,0:T(8,128)}), f32[64,768]{1,0:T(8,128)}) %reduce-scatter.15.cloned.1.call-update) | async-done | bytes 196624 | tf_op jit(solution)/shard_map/reduce_scatter | solution.py:293
  (249 shorter events, 41.8 us)
Async XLA Ops:
  7.2 49.6 %copy-start = (bf16[384,2048]{1,0:T(8,128)(2,1)S(1)}, bf16[384,2048]{1,0:T(8,128)(2,1)}, u32[]{:S(2)}) copy-start(bf16[384,2048]{1,0:T(8,128)(2,1)} %param.34) | copy-start | bytes 4718596
  7.2 4.3 copy-start.64
  7.2 348.8 %all-reduce.6.cloned.1.call-start = ((), (), s32[]{:S(2)}) async-start(), calls=%async_computation.8 | async-start | bytes 16777216 | tf_op jit(solution)/shard_map/psum | solution.py:173
  7.3 4.3 copy-start.8
  7.3 27.2 %copy-start.54 = (s32[6]{0:T(128)}, s32[6]{0:T(128)S(1)}, u32[]{:S(2)}) copy-start(s32[6]{0:T(128)S(1)} %fusion.88) | copy-start | bytes 76
  8.2 16.5 %copy-start.52 = (f32[2048]{0:T(1024)}, f32[2048]{0:T(1024)S(1)}, u32[]{:S(2)}) copy-start(f32[2048]{0:T(1024)S(1)} %convert_element_type.146) | copy-start | bytes 24580
  11.5 13.2 %copy-start.59 = (f32[1024]{0:T(1024)}, f32[1024]{0:T(1024)S(1)}, u32[]{:S(2)}) copy-start(f32[1024]{0:T(1024)S(1)} %add_rsqrt_fusion.3) | copy-start | bytes 12292
  11.6 27.6 %copy-start.61 = (f32[64]{0:T(128)}, f32[64]{0:T(128)S(1)}, u32[]{:S(2)}) copy-start(f32[64]{0:T(128)S(1)} %convert_element_type.151) | copy-start | bytes 772
  11.6 3.7 copy-start.66
  15.1 24.2 %copy-start.10 = (f32[1024,384]{0,1:T(8,128)}, f32[1024,384]{0,1:T(8,128)S(1)}, u32[]{:S(2)}) copy-start(f32[1024,384]{0,1:T(8,128)S(1)} %fusion.103) | copy-start | bytes 4718596
  15.3 23.9 %copy-start.45 = (f32[1024,6]{0,1:T(8,128)}, f32[1024,6]{0,1:T(8,128)S(1)}, u32[]{:S(2)}) copy-start(f32[1024,6]{0,1:T(8,128)S(1)} %add_rsqrt_fusion.1) | copy-start | bytes 73732
  15.3 23.9 %copy-start.56 = (f32[64]{0:T(128)}, f32[64]{0:T(128)S(1)}, u32[]{:S(2)}) copy-start(f32[64]{0:T(128)S(1)} %convert_element_type.153) | copy-start | bytes 772
  29.2 4.9 copy-start.63
  34.1 6.3 copy-start.47
  34.3 4.9 copy-start.5
  37.4 9.1 copy-start.23
  37.4 16.6 %copy-start.36 = (bf16[512,6,64]{0,1,2:T(8,128)(2,1)}, bf16[512,6,64]{0,1,2:T(8,128)(2,1)S(1)}, u32[]{:S(2)}) copy-start(bf16[512,6,64]{0,1,2:T(8,128)(2,1)S(1)} %slice.197) | copy-start | bytes 1179652
  41.0 10.9 copy-start.15
  41.0 10.9 copy-start.17
  41.0 10.9 copy-start.19
  41.0 10.9 copy-start.21
  43.5 4.5 copy-start.1
  62.5 640.7 %all-reduce.8.cloned.1.call-start = ((), (), s32[]{:S(2)}) async-start(), calls=%async_computation.10 | async-start | bytes 16777216 | tf_op jit(solution)/shard_map/psum | solution.py:203
  361.7 3.2 copy-start.2
  361.7 14.6 %slice-start.7 = ((s8[4718592]{0:T(1024)(128)(4,1)}), s8[524288]{0:T(1024)(128)(4,1)S(1)}, s32[]{:S(2)}) async-start(s8[4718592]{0:T(1024)(128)(4,1)} %bitcast.161), calls=%async_computation.25 | async-start | bytes 1048576
  364.9 11.4 copy-start.29
  364.9 11.4 slice-start.8
  376.3 7.4 copy-start.27
  376.4 20.1 %slice-start.5 = ((s8[4718592]{0:T(1024)(128)(4,1)}), s8[4194304]{0:T(1024)(128)(4,1)S(1)}, s32[]{:S(2)}) async-start(s8[4718592]{0:T(1024)(128)(4,1)} %bitcast.159), calls=%async_computation.23 | async-start | bytes 8388608
  376.4 28.3 %slice-start.9 = ((s8[4718592]{0:T(1024)(128)(4,1)}), s8[4194304]{0:T(1024)(128)(4,1)S(1)}, s32[]{:S(2)}) async-start(s8[4718592]{0:T(1024)(128)(4,1)} %bitcast.163), calls=%async_computation.27 | async-start | bytes 8388608
  383.7 12.7 %slice-start.6 = ((s8[4718592]{0:T(1024)(128)(4,1)}), s8[524288]{0:T(1024)(128)(4,1)S(1)}, s32[]{:S(2)}) async-start(s8[4718592]{0:T(1024)(128)(4,1)} %bitcast.159), calls=%async_computation.24 | async-start | bytes 1048576
  383.7 20.9 %slice-start.10 = ((s8[4718592]{0:T(1024)(128)(4,1)}), s8[524288]{0:T(1024)(128)(4,1)S(1)}, s32[]{:S(2)}) async-start(s8[4718592]{0:T(1024)(128)(4,1)} %bitcast.163), calls=%async_computation.28 | async-start | bytes 1048576
  396.5 8.2 copy-start.68
  413.2 442.8 %reduce-scatter.19.cloned.1.call-start = ((), (), s32[]{:S(2)}) async-start(), calls=%async_computation.15 | async-start | bytes 5308416 | tf_op jit(solution)/shard_map/reduce_scatter | solution.py:283
  422.9 435.3 %reduce-scatter.21.cloned.1.call-start = ((), (), s32[]{:S(2)}) async-start(), calls=%async_computation.16 | async-start | bytes 5308416 | tf_op jit(solution)/shard_map/reduce_scatter | solution.py:286
  432.5 441.0 %reduce-scatter.23.cloned.1.call-start = ((), (), s32[]{:S(2)}) async-start(), calls=%async_computation.17 | async-start | bytes 5308416 | tf_op jit(solution)/shard_map/reduce_scatter | solution.py:289
  441.8 510.8 %reduce-scatter.9.cloned.1.call-start = ((), (), s32[]{:S(2)}) async-start(), calls=%async_computation.9 | async-start | bytes 5242880 | tf_op jit(solution)/shard_map/reduce_scatter | solution.py:183
  442.5 284.9 %copy-start.50 = (f32[6,512]{1,0:T(8,128)}, f32[6,512]{1,0:T(8,128)S(1)}, u32[]{:S(2)}) copy-start(f32[6,512]{1,0:T(8,128)S(1)} %log_add_fusion.1) | copy-start | bytes 36868
  452.0 542.7 %reduce-scatter.13.cloned.1.call-start = ((), (), s32[]{:S(2)}) async-start(), calls=%async_computation.12 | async-start | bytes 1769472 | tf_op jit(solution)/shard_map/reduce_scatter | solution.py:277
  703.2 8.5 copy-start.7
  703.2 9.9 copy-start.28
  710.1 17.3 %slice-start.3 = ((s8[6291456]{0:T(1024)(128)(4,1)}), s8[4194304]{0:T(1024)(128)(4,1)S(1)}, s32[]{:S(2)}) async-start(s8[6291456]{0:T(1024)(128)(4,1)} %bitcast.132), calls=%async_computation.21 | async-start | bytes 8388608
  713.0 14.3 %slice-start.4 = ((s8[6291456]{0:T(1024)(128)(4,1)}), s8[2097152]{0:T(1024)(128)(4,1)S(1)}, s32[]{:S(2)}) async-start(s8[6291456]{0:T(1024)(128)(4,1)} %bitcast.132), calls=%async_computation.22 | async-start | bytes 4194304
  721.3 6.1 copy-start.37
  727.4 4.8 copy-start.30
  732.1 10.4 slice-start
  732.1 10.4 slice-start.1
  736.9 5.6 slice-start.2
  736.9 5.6 copy-start.24
  736.9 5.6 copy-start.32
  748.9 6.9 copy-start.18
  748.9 6.9 copy-start.35
  761.8 7.0 copy-start.43
  761.8 3.0 copy-start.31
  761.8 3.0 copy-start.51
  765.9 2.9 copy-start.9
  765.9 2.9 copy-start.53
  765.9 2.9 copy-start.60
  768.8 5.4 copy-start.41
  774.2 3.7 copy-start.14
  779.3 257.2 %reduce-scatter.17.cloned.1.call-start = ((), (), s32[]{:S(2)}) async-start(), calls=%async_computation.14 | async-start | bytes 1769472 | tf_op jit(solution)/shard_map/reduce_scatter | solution.py:280
  785.7 2.8 copy-start.55
  785.7 329.8 %reduce-scatter.11.cloned.1.call-start = ((), (), s32[]{:S(2)}) async-start(), calls=%async_computation.11 | async-start | bytes 5242880 | tf_op jit(solution)/shard_map/reduce_scatter | solution.py:271
  799.9 437.2 %reduce-scatter.15.cloned.1.call-start = ((), (), s32[]{:S(2)}) async-start(), calls=%async_computation.13 | async-start | bytes 6488064 | tf_op jit(solution)/shard_map/reduce_scatter | solution.py:293
  (26 other events, 43.4 us)
Sparse Core Ops, SparseCore 0:
  62.6 293.3 all-reduce.5
  413.3 289.8 all-reduce.7
  706.6 52.7 reduce-scatter.18
  762.7 53.7 reduce-scatter.20
  819.9 53.6 reduce-scatter.22
  875.7 76.7 reduce-scatter.8
  955.8 38.8 reduce-scatter.12
  998.0 38.3 reduce-scatter.16
  1038.7 76.7 reduce-scatter.10
  1121.6 115.4 reduce-scatter.14
where the time goes:
time: 1250 us; the launch traced here: 1240 us
  waiting for transfers between devices  863 us (69%)
  matrix products  172 us (14%)
  other arithmetic  80.4 us (6%)
  local copies, waits for them, and re-layouts  71.4 us (6%)
  blocking collectives  41.1 us (3%)
  between operations  15.7 us (1%)
    psum x1, waiting for transfers between devices, shards(): hidden_full = x_float + lax.psum(attn_part, 'mp')  293 us
    psum x1, waiting for transfers between devices, shards(): dn_two = lax.psum(dn_two_part, 'mp')  251 us
    reduce_scatter x1, waiting for transfers between devices, shards(): lax.psum_scatter(dn_one_part.astype(jnp.bfloat16), 'mp', scatter_dimensio...  77.4 us
    reduce_scatter x1, waiting for transfers between devices, shards(): lax.psum_scatter(ffn_part.astype(jnp.bfloat16), 'mp', scatter_dimension=0...  76.7 us
    reduce_scatter x1, waiting for transfers between devices, shards(): lax.psum_scatter(grad_keyval, ('dp', 'mp'), scatter_dimension=0, tiled=True)  73.2 us
    psum x1, blocking collectives, shards(): lax.psum((grad_gain_one, grad_gain_two, grad_q_gain, grad_k_gain), ('dp',...  41.1 us
    reduce_scatter x1, waiting for transfers between devices, shards(): lax.psum_scatter(grad_out_proj.astype(jnp.bfloat16), 'dp', scatter_dimens...  39.9 us
    reduce_scatter x1, waiting for transfers between devices, shards(): lax.psum_scatter(grad_query.astype(jnp.bfloat16), 'dp', scatter_dimension...  38.2 us
  transfers between devices with their start and end apart: 10, of which 8 were waited for; matrix products, arithmetic and copies ran while one was open for 16% of the time, Pallas kernels for 0%

commit v1 on v0

--- a/solution.py
+++ b/solution.py
@@ -170,7 +170,7 @@
         jnp.concatenate(block_outs, axis=0).reshape(row_count, head_span).astype(jnp.bfloat16)
     )
     attn_part = jnp.dot(attended, w_out, preferred_element_type=jnp.float32)
-    hidden_full = x_float + lax.psum(attn_part, "mp")
+    hidden_full = x_float + jnp.sum(lax.all_gather(attn_part, "mp"), axis=0)
     hidden_rows = lax.dynamic_slice_in_dim(hidden_full, row_first, shard_rows, 0)
     xn_two = (normalize(hidden_full) * gain_two).astype(jnp.bfloat16)
     live_cols = jnp.repeat(slot_live.astype(jnp.float32), tile_cols)

time: 1250 us -> 1530 us (1.22)
  waiting for transfers between devices: 863 us -> 1130 us
  other arithmetic: 80.4 us -> 96.9 us
    all_gather x0 -> x1, waiting for transfers between devices: none -> 563 us  [shards(): hidden_full = x_float + jnp.sum(lax.all_gather(attn_part, 'mp'), axis=0)]
    psum x1 -> x0, waiting for transfers between devices: 293 us -> none  [shards(): hidden_full = x_float + lax.psum(attn_part, 'mp')]
    reduce_sum x0 -> x1, other arithmetic: none -> 16.4 us  [shards(): hidden_full = x_float + jnp.sum(lax.all_gather(attn_part, 'mp'), axis=0)]
  transfers between devices with their start and end apart: 10 -> 10, of which waited for: 8 -> 8; matrix products, arithmetic and copies ran while one was open for 16% -> 13% of each run, Pallas kernels for 0% -> 0%
where the time goes in v1:
time: 1530 us
  waiting for transfers between devices  1130 us (74%)
  matrix products  171 us (11%)
  other arithmetic  96.9 us (6%)
  local copies, waits for them, and re-layouts  71.2 us (5%)
  blocking collectives  41.1 us (3%)
  between operations  15.7 us (1%)
    all_gather x1, waiting for transfers between devices, shards(): hidden_full = x_float + jnp.sum(lax.all_gather(attn_part, 'mp'), axis=0)  563 us
    psum x1, waiting for transfers between devices, shards(): dn_two = lax.psum(dn_two_part, 'mp')  250 us
    reduce_scatter x1, waiting for transfers between devices, shards(): lax.psum_scatter(dn_one_part.astype(jnp.bfloat16), 'mp', scatter_dimensio...  77.4 us
    reduce_scatter x1, waiting for transfers between devices, shards(): lax.psum_scatter(ffn_part.astype(jnp.bfloat16), 'mp', scatter_dimension=0...  76.7 us
    reduce_scatter x1, waiting for transfers between devices, shards(): lax.psum_scatter(grad_keyval, ('dp', 'mp'), scatter_dimension=0, tiled=True)  73.2 us
    psum x1, blocking collectives, shards(): lax.psum((grad_gain_one, grad_gain_two, grad_q_gain, grad_k_gain), ('dp',...  41.1 us
    reduce_scatter x1, waiting for transfers between devices, shards(): lax.psum_scatter(grad_out_proj.astype(jnp.bfloat16), 'dp', scatter_dimens...  39.9 us
    reduce_scatter x1, waiting for transfers between devices, shards(): lax.psum_scatter(grad_query.astype(jnp.bfloat16), 'dp', scatter_dimension...  38.1 us
  transfers between devices with their start and end apart: 10, of which 8 were waited for; matrix products, arithmetic and copies ran while one was open for 13% of the time, Pallas kernels for 0%

profile of v1, /device:TPU:0, one launch (start us, length us, event | category | flops | bytes accessed | tf_op | source)
XLA Modules:
  0.0 1529.2 jit_solution(7573559613667876894)
XLA Ops:
  8.2 3.3 multiply_reduce_fusion.3
  11.6 3.5 fusion.103
  15.3 4.5 constant_dynamic-slice_fusion.1
  19.9 2.3 copy.165
  22.2 2.2 copy.164
  24.4 4.5 fusion.45
  34.2 2.9 fusion.58
  40.7 2.4 fusion.108
  43.2 3.0 fusion
  47.7 3.6 fusion.68
  56.5 5.7 fusion.110
  62.9 563.3 %all-gather.3.cloned.1.call-done = f32[4096,2048]{1,0:T(8,128)} async-done(((f32[1024,2048]{1,0:T(8,128)}), f32[4096,2048]{1,0:T(8,128)}) %all-gather.3.cloned.1.call-update) | async-done | bytes 33554448 | tf_op jit(solution)/shard_map/all_gather | solution.py:173
  626.3 16.4 %reduce_sum.215 = f32[1024,2048]{1,0:T(8,128)} reduce(f32[4,1024,2048]{2,1,0:T(8,128)} %bitcast.135, f32[]{:T(128)} %constant.179.clone.1), dimensions={0}, to_apply=%region_10.11 | reduce | flops 6291456 | bytes 41943044 | tf_op jit(solution)/shard_map/reduce_sum | solution.py:173
  642.7 5.7 multiply_reduce_fusion.2
  649.2 2.4 copy-done.2
  651.6 11.0 fusion.111
  662.7 7.3 fusion.112
  670.0 12.8 multiply_convert_fusion.4
  682.9 8.1 fusion.113
  691.1 8.0 convolution_add_fusion
  699.1 9.6 convolution_convert_fusion.2
  708.8 9.6 convolution_convert_fusion.1
  718.5 9.3 convolution_convert_fusion
  728.5 9.5 convolution_convert_fusion.3
  738.1 250.1 %all-reduce.5.cloned.1.call-done = f32[1024,2048]{1,0:T(8,128)} async-done(((f32[1024,2048]{1,0:T(8,128)}), f32[1024,2048]{1,0:T(8,128)}) %all-reduce.5.cloned.1.call-update) | async-done | bytes 8388624 | tf_op jit(solution)/shard_map/psum | solution.py:203
  988.3 6.7 multiply_reduce_fusion.1
  998.1 8.3 multiply_add_fusion
  1006.4 5.3 fusion.55
  1012.5 4.8 multiply_reduce_fusion.4
  1017.3 4.8 multiply_convert_fusion.3
  1022.1 2.7 fusion.64
  1024.7 2.9 fusion.62
  1027.7 6.3 multiply_reduce_fusion
  1034.0 7.1 multiply_convert_fusion
  1042.4 2.1 fusion.63
  1051.3 2.5 fusion.49
  1053.8 5.3 fusion.73
  1059.2 3.7 copy-done.14
  1064.3 6.3 convolution_convert_fusion.6
  1070.7 2.8 copy.152
  1077.5 7.4 fusion.19
  1085.2 5.2 fusion.104
  1090.5 3.7 fusion.26
  1096.9 5.7 fusion.29
  1103.5 1.8 copy.158
  1105.3 3.0 broadcast_in_dim.37
  1108.3 11.5 dynamic_update_slice.6
  1119.8 11.0 dynamic_update_slice.7
  1130.9 6.5 convert_element_type.145
  1137.4 1.8 multiply_reduce_fusion.7
  1139.2 1.8 multiply_reduce_fusion.6
  1141.1 2.2 convert_element_type.185
  1143.2 2.2 convert_element_type.187
  1145.4 13.2 reduce-scatter.23.cloned.1.call-done
  1158.6 2.2 convert_element_type.189
  1160.9 76.7 %reduce-scatter.9.cloned.1.call-done = bf16[256,2048]{1,0:T(8,128)(2,1)} async-done(((bf16[1024,2048]{1,0:T(8,128)(2,1)}), bf16[256,2048]{1,0:T(8,128)(2,1)}) %reduce-scatter.9.cloned.1.call-update) | async-done | bytes 1048592 | tf_op jit(solution)/shard_map/reduce_scatter | solution.py:183
  1237.6 4.0 multiply_reduce_fusion.5
  1241.6 38.1 %reduce-scatter.13.cloned.1.call-done = bf16[256,384]{0,1:T(8,128)(2,1)} async-done(((bf16[2048,384]{0,1:T(8,128)(2,1)}), bf16[256,384]{0,1:T(8,128)(2,1)}) %reduce-scatter.13.cloned.1.call-update) | async-done | bytes 196624 | tf_op jit(solution)/shard_map/reduce_scatter | solution.py:277
  1281.6 39.9 %reduce-scatter.17.cloned.1.call-done = bf16[384,256]{1,0:T(8,128)(2,1)} async-done(((bf16[384,2048]{1,0:T(8,128)(2,1)}), bf16[384,256]{1,0:T(8,128)(2,1)}) %reduce-scatter.17.cloned.1.call-update) | async-done | bytes 196624 | tf_op jit(solution)/shard_map/reduce_scatter | solution.py:280
  1323.1 77.4 %reduce-scatter.11.cloned.1.call-done = bf16[256,2048]{1,0:T(8,128)(2,1)} async-done(((bf16[1024,2048]{1,0:T(8,128)(2,1)}), bf16[256,2048]{1,0:T(8,128)(2,1)}) %reduce-scatter.11.cloned.1.call-update) | async-done | bytes 1048592 | tf_op jit(solution)/shard_map/reduce_scatter | solution.py:271
  1400.5 2.7 fusion.39
  1403.2 41.1 %all-reduce.2 = (f32[2048]{0:T(1024)}, f32[64]{0:T(128)}, f32[64]{0:T(128)}, f32[2048]{0:T(1024)}) all-reduce(f32[2048]{0:T(1024)S(1)} %get-tuple-element.124, f32[64]{0:T(128)S(1)} %reduce_sum.227, f32[64]{0:T(128)S(1)} %get-tuple-element.126, f32[2048]{0:T(1024)S(1)} %get-tuple-element.141), channel_id=1, replica_groups=mesh['dp'=8,'mp'=4] {'dp','mp'}, use_global_device_ids=true, to_apply=%region_23.24 | all-reduce | flops 4224 | bytes 33792 | tf_op jit(solution)/shard_map/psum | solution.py:294
  1444.3 4.6 fusion.38
  1448.9 73.2 %reduce-scatter.15.cloned.1.call-done = f32[64,768]{1,0:T(8,128)} async-done(((f32[2048,768]{1,0:T(8,128)}), f32[64,768]{1,0:T(8,128)}) %reduce-scatter.15.cloned.1.call-update) | async-done | bytes 196624 | tf_op jit(solution)/shard_map/reduce_scatter | solution.py:293
  (250 shorter events, 43.8 us)
Async XLA Ops:
  7.2 49.3 %copy-start = (bf16[384,2048]{1,0:T(8,128)(2,1)S(1)}, bf16[384,2048]{1,0:T(8,128)(2,1)}, u32[]{:S(2)}) copy-start(bf16[384,2048]{1,0:T(8,128)(2,1)} %param.34) | copy-start | bytes 4718596
  7.2 4.3 copy-start.64
  7.2 619.0 %all-gather.3.cloned.1.call-start = ((), (), s32[]{:S(2)}) async-start(), calls=%async_computation.17 | async-start | bytes 41943040 | tf_op jit(solution)/shard_map/all_gather | solution.py:173
  7.3 4.3 copy-start.8
  7.3 26.9 %copy-start.54 = (s32[6]{0:T(128)}, s32[6]{0:T(128)S(1)}, u32[]{:S(2)}) copy-start(s32[6]{0:T(128)S(1)} %fusion.88) | copy-start | bytes 76
  8.2 16.2 %copy-start.52 = (f32[2048]{0:T(1024)}, f32[2048]{0:T(1024)S(1)}, u32[]{:S(2)}) copy-start(f32[2048]{0:T(1024)S(1)} %convert_element_type.146) | copy-start | bytes 24580
  11.5 12.9 copy-start.59
  11.6 27.4 %copy-start.61 = (f32[64]{0:T(128)}, f32[64]{0:T(128)S(1)}, u32[]{:S(2)}) copy-start(f32[64]{0:T(128)S(1)} %convert_element_type.151) | copy-start | bytes 772
  11.6 3.7 copy-start.66
  15.1 23.9 %copy-start.10 = (f32[1024,384]{0,1:T(8,128)}, f32[1024,384]{0,1:T(8,128)S(1)}, u32[]{:S(2)}) copy-start(f32[1024,384]{0,1:T(8,128)S(1)} %fusion.103) | copy-start | bytes 4718596
  15.3 23.6 %copy-start.45 = (f32[1024,6]{0,1:T(8,128)}, f32[1024,6]{0,1:T(8,128)S(1)}, u32[]{:S(2)}) copy-start(f32[1024,6]{0,1:T(8,128)S(1)} %add_rsqrt_fusion.1) | copy-start | bytes 73732
  15.3 23.6 %copy-start.56 = (f32[64]{0:T(128)}, f32[64]{0:T(128)S(1)}, u32[]{:S(2)}) copy-start(f32[64]{0:T(128)S(1)} %convert_element_type.153) | copy-start | bytes 772
  29.0 4.9 copy-start.63
  33.8 6.3 copy-start.47
  34.0 4.9 copy-start.5
  37.1 9.2 copy-start.23
  37.1 16.6 %copy-start.36 = (bf16[512,6,64]{0,1,2:T(8,128)(2,1)}, bf16[512,6,64]{0,1,2:T(8,128)(2,1)S(1)}, u32[]{:S(2)}) copy-start(bf16[512,6,64]{0,1,2:T(8,128)(2,1)S(1)} %slice.197) | copy-start | bytes 1179652
  40.7 10.9 copy-start.15
  40.7 10.9 copy-start.17
  40.7 10.9 copy-start.19
  40.7 10.9 copy-start.21
  43.2 4.5 copy-start.1
  52.8 2.6 copy-start.3
  62.2 926.1 %all-reduce.5.cloned.1.call-start = ((), (), s32[]{:S(2)}) async-start(), calls=%async_computation.9 | async-start | bytes 16777216 | tf_op jit(solution)/shard_map/psum | solution.py:203
  648.4 3.2 copy-start.2
  648.4 14.2 slice-start.7
  651.6 11.0 copy-start.29
  651.6 11.0 slice-start.8
  662.7 7.3 copy-start.27
  662.7 20.2 %slice-start.5 = ((s8[4718592]{0:T(1024)(128)(4,1)}), s8[4194304]{0:T(1024)(128)(4,1)S(1)}, s32[]{:S(2)}) async-start(s8[4718592]{0:T(1024)(128)(4,1)} %bitcast.161), calls=%async_computation.23 | async-start | bytes 8388608
  662.7 28.3 %slice-start.9 = ((s8[4718592]{0:T(1024)(128)(4,1)}), s8[4194304]{0:T(1024)(128)(4,1)S(1)}, s32[]{:S(2)}) async-start(s8[4718592]{0:T(1024)(128)(4,1)} %bitcast.165), calls=%async_computation.27 | async-start | bytes 8388608
  670.0 12.9 slice-start.6
  670.0 21.0 %slice-start.10 = ((s8[4718592]{0:T(1024)(128)(4,1)}), s8[524288]{0:T(1024)(128)(4,1)S(1)}, s32[]{:S(2)}) async-start(s8[4718592]{0:T(1024)(128)(4,1)} %bitcast.165), calls=%async_computation.28 | async-start | bytes 1048576
  682.9 8.2 copy-start.68
  699.1 442.0 %reduce-scatter.19.cloned.1.call-start = ((), (), s32[]{:S(2)}) async-start(), calls=%async_computation.14 | async-start | bytes 5308416 | tf_op jit(solution)/shard_map/reduce_scatter | solution.py:283
  708.8 434.5 %reduce-scatter.21.cloned.1.call-start = ((), (), s32[]{:S(2)}) async-start(), calls=%async_computation.15 | async-start | bytes 5308416 | tf_op jit(solution)/shard_map/reduce_scatter | solution.py:286
  718.4 440.2 %reduce-scatter.23.cloned.1.call-start = ((), (), s32[]{:S(2)}) async-start(), calls=%async_computation.16 | async-start | bytes 5308416 | tf_op jit(solution)/shard_map/reduce_scatter | solution.py:289
  727.8 509.8 %reduce-scatter.9.cloned.1.call-start = ((), (), s32[]{:S(2)}) async-start(), calls=%async_computation.8 | async-start | bytes 5242880 | tf_op jit(solution)/shard_map/reduce_scatter | solution.py:183
  728.5 284.0 %copy-start.50 = (f32[6,512]{1,0:T(8,128)}, f32[6,512]{1,0:T(8,128)S(1)}, u32[]{:S(2)}) copy-start(f32[6,512]{1,0:T(8,128)S(1)} %log_add_fusion.1) | copy-start | bytes 36868
  738.1 541.7 %reduce-scatter.13.cloned.1.call-start = ((), (), s32[]{:S(2)}) async-start(), calls=%async_computation.11 | async-start | bytes 1769472 | tf_op jit(solution)/shard_map/reduce_scatter | solution.py:277
  988.3 8.5 copy-start.7
  988.3 9.9 copy-start.28
  995.0 17.4 %slice-start.3 = ((s8[6291456]{0:T(1024)(128)(4,1)}), s8[4194304]{0:T(1024)(128)(4,1)S(1)}, s32[]{:S(2)}) async-start(s8[6291456]{0:T(1024)(128)(4,1)} %bitcast.133), calls=%async_computation.21 | async-start | bytes 8388608
  998.1 14.3 slice-start.4
  1006.4 6.1 copy-start.37
  1012.5 4.8 copy-start.30
  1017.2 10.4 slice-start
  1017.3 10.4 slice-start.1
  1022.0 2.7 copy-start.16
  1022.0 5.6 slice-start.2
  1022.0 5.6 copy-start.24
  1022.1 5.6 copy-start.32
  1034.0 7.1 copy-start.18
  1034.0 7.1 copy-start.35
  1047.1 6.7 copy-start.43
  1047.1 3.0 copy-start.31
  1047.1 3.0 copy-start.51
  1053.8 5.4 copy-start.41
  1059.2 3.7 copy-start.14
  1064.3 257.1 %reduce-scatter.17.cloned.1.call-start = ((), (), s32[]{:S(2)}) async-start(), calls=%async_computation.13 | async-start | bytes 1769472 | tf_op jit(solution)/shard_map/reduce_scatter | solution.py:280
  1070.7 2.8 copy-start.26
  1070.7 2.8 copy-start.55
  1070.7 329.9 %reduce-scatter.11.cloned.1.call-start = ((), (), s32[]{:S(2)}) async-start(), calls=%async_computation.10 | async-start | bytes 5242880 | tf_op jit(solution)/shard_map/reduce_scatter | solution.py:271
  1085.0 437.1 %reduce-scatter.15.cloned.1.call-start = ((), (), s32[]{:S(2)}) async-start(), calls=%async_computation.12 | async-start | bytes 6488064 | tf_op jit(solution)/shard_map/reduce_scatter | solution.py:293
  (26 other events, 43.0 us)
Sparse Core Ops, SparseCore 0:
  62.3 563.9 all-gather.2
  699.2 289.0 all-reduce.4
  991.7 52.7 reduce-scatter.18
  1047.8 53.7 reduce-scatter.20
  1104.9 53.6 reduce-scatter.22
  1160.8 76.7 reduce-scatter.8
  1240.9 38.8 reduce-scatter.12
  1283.0 38.3 reduce-scatter.16
  1323.7 76.7 reduce-scatter.10
  1406.6 115.4 reduce-scatter.14
